TPU v7x, 8 devices: a whole 2x2x1 slice. The times are simulated.
8 devices in a mesh: fsdp: 8 (over z, y, x, core).
Axes of the slice: x: 2, y: 2, z: 1, core: 2. Of those that a mesh axis runs over, the one named last changes fastest.
Arguments:
- acts_in: bfloat16 [4, 32768, 768], P(None, 'fsdp')
- cot_out: bfloat16 [4, 32768, 768], P(None, 'fsdp')
- w_in: bfloat16 [2, 768, 3072], P(None, 'fsdp')
- w_out: bfloat16 [2, 3072, 768], P(None, 'fsdp')
Outputs:
- output 1: float32 [2, 768, 3072], P(None, 'fsdp')
- output 2: float32 [2, 3072, 768], P(None, 'fsdp')
All inputs are finite; a program needn't handle non-finite values.
Results may differ from a plain program's by a relative error of at most 0.011845.
Values are sent between devices in bfloat16 or wider.
A program may use at most 1 GiB of HBM per device.

v0:
```python
import math
import jax
import jax.numpy as jnp
from jax import lax
from jax.sharding import PartitionSpec as P

GROUP_AXIS = "fsdp"


def gelu_pair(hidden):
    h_float = hidden.astype(jnp.float32)
    gelu_coeff = math.sqrt(2.0 / math.pi)
    tanh_val = jnp.tanh(gelu_coeff * (h_float + 0.044715 * h_float * h_float * h_float))
    gelu_value = 0.5 * h_float * (1.0 + tanh_val)
    gelu_slope = 0.5 * (1.0 + tanh_val) + 0.5 * h_float * (1.0 - tanh_val * tanh_val) * gelu_coeff * (1.0 + 3.0 * 0.044715 * h_float * h_float)
    return gelu_value.astype(jnp.bfloat16), gelu_slope


def solution(mesh):
    row_spec = P(None, GROUP_AXIS, None)
    contract_cols = (((1,), (1,)), ((), ()))
    contract_rows = (((0,), (0,)), ((), ()))

    def local_run(acts_loc, cot_loc, w_in_loc, w_out_loc):
        num_layers = w_in_loc.shape[0]

        def micro_body(acc_pair, xs_pair):
            acc_in, acc_out = acc_pair
            x_cur, grad_x = xs_pair
            saved_acts = []
            for layer_idx in range(num_layers):
                w_in_full = lax.all_gather(w_in_loc[layer_idx], GROUP_AXIS, axis=0, tiled=True)
                w_out_full = lax.all_gather(w_out_loc[layer_idx], GROUP_AXIS, axis=0, tiled=True)
                hidden = jnp.dot(x_cur, w_in_full, preferred_element_type=jnp.float32).astype(jnp.bfloat16)
                saved_acts.append((x_cur, hidden))
                x_cur = x_cur + jnp.dot(gelu_pair(hidden)[0], w_out_full, preferred_element_type=jnp.float32).astype(jnp.bfloat16)
            new_in = list(acc_in)
            new_out = list(acc_out)
            for layer_idx in reversed(range(num_layers)):
                x_saved, hidden = saved_acts[layer_idx]
                active, gelu_slope = gelu_pair(hidden)
                w_out_full = lax.all_gather(w_out_loc[layer_idx], GROUP_AXIS, axis=0, tiled=True)
                grad_act = lax.dot_general(grad_x, w_out_full, contract_cols, preferred_element_type=jnp.float32).astype(jnp.bfloat16)
                grad_hid = (grad_act.astype(jnp.float32) * gelu_slope).astype(jnp.bfloat16)
                part_out = lax.dot_general(active, grad_x, contract_rows, preferred_element_type=jnp.float32)
                part_in = lax.dot_general(x_saved, grad_hid, contract_rows, preferred_element_type=jnp.float32)
                if layer_idx > 0:
                    w_in_full = lax.all_gather(w_in_loc[layer_idx], GROUP_AXIS, axis=0, tiled=True)
                    grad_x = (grad_x.astype(jnp.float32) + lax.dot_general(grad_hid, w_in_full, contract_cols, preferred_element_type=jnp.float32)).astype(jnp.bfloat16)
                new_out[layer_idx] = acc_out[layer_idx] + lax.psum_scatter(part_out, GROUP_AXIS, scatter_dimension=0, tiled=True)
                new_in[layer_idx] = acc_in[layer_idx] + lax.psum_scatter(part_in, GROUP_AXIS, scatter_dimension=0, tiled=True)
            return (tuple(new_in), tuple(new_out)), None

        zero_in = tuple(jnp.zeros(w_in_loc.shape[1:], jnp.float32) for layer_idx in range(num_layers))
        zero_out = tuple(jnp.zeros(w_out_loc.shape[1:], jnp.float32) for layer_idx in range(num_layers))
        final_acc, unused_ys = lax.scan(micro_body, (zero_in, zero_out), (acts_loc, cot_loc))
        return jnp.stack(final_acc[0]), jnp.stack(final_acc[1])

    return jax.shard_map(local_run, mesh=mesh, in_specs=(row_spec, row_spec, row_spec, row_spec), out_specs=(row_spec, row_spec), check_vma=False)
```

profile of v0, /device:TPU:0, one launch (start us, length us, event | category | flops | bytes accessed | tf_op | source)
XLA Modules:
  0.0 1986.6 jit_solution(2365129737674411482)
XLA Ops:
  7.2 1966.1 %while.17 = (s32[]{:T(128)}, f32[96,3072]{1,0:T(8,128)}, f32[96,3072]{1,0:T(8,128)}, f32[384,768]{1,0:T(8,128)}, f32[384,768]{1,0:T(8,128)}, /*index=5*/bf16[4,4...) while((s32[]{:T(128)}, f32[96,3072]{1,0:T(8,128)}, ...), condition=%wide.region_5.6_spmd.clone, body=%wide.region_0.5_spmd.clone.sunk | while | flops 194247917568 | bytes 707002816 | solution.py:56
  13.7 32.2 %all-gather.21.cloned.1.call-done = bf16[1,768,3072]{2,1,0:T(8,128)(2,1)} async-done(((bf16[1,96,3072]{2,1,0:T(8,128)(2,1)}), bf16[1,768,3072]{2,1,0:T(8,128)(2,1)}) %all-gather.21.cloned.1.call-update) | async-done | bytes 4718608 | tf_op jit(solution)/shard_map/while/body/eval_jaxpr/all_gather | solution.py:32
  45.9 26.9 %convolution_convert_fusion.5 = bf16[4096,3072]{1,0:T(8,128)(2,1)} fusion(bf16[4,4096,768]{2,1,0:T(8,128)(2,1)} %get-tuple-element.198, s32[]{:T(128)S(6)} %copy.11, bf16[1,768,3072]{2,1,0:T(8,128)(2,1)} %all-gather.21.cloned.1.call-done), kind=kOutput, calls=%fused_computation.40.clone.1 | convolution fusion | flops 19339935744 | bytes 36175876 | tf_op jit(solution)/shard_map/while/body/eval_jaxpr/dot_general | solution.py:34
  80.6 37.0 %bitcast_add_fusion.2 = bf16[4096,768]{1,0:T(8,128)(2,1)} fusion(bf16[4,4096,768]{2,1,0:T(8,128)(2,1)} %get-tuple-element.198, s32[]{:T(128)S(6)} %copy.11, bf16[1,3072,768]{2,1,0:T(8,128)(2,1)} %all-gather.23.cloned.1.call-done, bf16[4096,3072]{1,0:T(8,128)(2,1)} %convolution_convert_fusion.5), kind=kOutput, calls=%fused_computation.46.clone.1 | convolution fusion | flops 19459473408 | bytes 42467332 | tf_op jit(solution)/shard_map/while/body/eval_jaxpr/dot_general | solution.py:36
  117.6 27.2 %convolution_convert_fusion.6 = bf16[4096,3072]{1,0:T(8,128)(2,1)} fusion(bf16[4096,768]{1,0:T(8,128)(2,1)} %bitcast_add_fusion.2, bf16[1,768,3072]{2,1,0:T(8,128)(2,1)} %all-gather.25.cloned.1.call-done), kind=kOutput, calls=%fused_computation.39.clone.1 | convolution fusion | flops 19339935744 | bytes 36175872 | tf_op jit(solution)/shard_map/while/body/eval_jaxpr/dot_general | solution.py:34
  144.8 33.4 %fusion.142 = f32[3072,768]{1,0:T(8,128)} fusion(bf16[4096,3072]{1,0:T(8,128)(2,1)} %convolution_convert_fusion.6, bf16[4,4096,768]{2,1,0:T(8,128)(2,1)} %get-tuple-element.199, s32[]{:T(128)S(6)} %copy.11), kind=kOutput, calls=%fused_computation.36.clone.1 | convolution fusion | flops 19453181952 | bytes 40894468 | tf_op jit(solution)/shard_map/while/body/eval_jaxpr/dot_general | solution.py:45
  178.4 50.6 %fusion.137 = bf16[4096,3072]{1,0:T(8,128)(2,1)} fusion(bf16[4096,3072]{1,0:T(8,128)(2,1)} %convolution_convert_fusion.6, bf16[4,4096,768]{2,1,0:T(8,128)(2,1)} %get-tuple-element.199, s32[]{:T(128)S(6)} %copy.11, bf16[1,3072,768]{2,1,0:T(8,128)(2,1)} %all-gather.27.cloned.1.call-done), kind=kOutput, calls=%fused_computation.22.clone.2 | convolution fusion | flops 19604176896 | bytes 61341700 | tf_op jit(solution)/shard_map/while/body/eval_jaxpr/dot_general | solution.py:43
  229.0 27.0 %fusion.140 = f32[768,3072]{1,0:T(8,128)} fusion(bf16[4096,768]{1,0:T(8,128)(2,1)} %bitcast_add_fusion.2, bf16[4096,3072]{1,0:T(8,128)(2,1)} %fusion.137), kind=kOutput, calls=%fused_computation.80.clone.1 | convolution fusion | flops 19327352832 | bytes 40894464 | tf_op jit(solution)/shard_map/while/body/eval_jaxpr/dot_general | solution.py:46
  281.3 51.2 %fusion.138 = bf16[4096,3072]{1,0:T(8,128)(2,1)} fusion(bf16[4096,3072]{1,0:T(8,128)(2,1)} %convolution_convert_fusion.5, bf16[4096,768]{1,0:T(8,128)(2,1)S(1)} %add_convert_fusion.2, bf16[1,3072,768]{2,1,0:T(8,128)(2,1)} %all-gather.23.cloned.1.call-done), kind=kOutput, calls=%fused_computation.29.clone.clone.2.clone.1 | convolution fusion | flops 19604176896 | bytes 61341696 | tf_op jit(solution)/shard_map/while/body/eval_jaxpr/dot_general | solution.py:43
  332.5 27.4 %fusion.139 = f32[768,3072]{1,0:T(8,128)} fusion(bf16[4,4096,768]{2,1,0:T(8,128)(2,1)} %get-tuple-element.198, s32[]{:T(128)S(6)} %copy.11, bf16[4096,3072]{1,0:T(8,128)(2,1)} %fusion.138), kind=kOutput, calls=%fused_computation.37.clone.3 | convolution fusion | flops 19327352832 | bytes 40894468 | tf_op jit(solution)/shard_map/while/body/eval_jaxpr/dot_general | solution.py:46
  359.9 33.4 %fusion.141 = f32[3072,768]{1,0:T(8,128)} fusion(bf16[4096,768]{1,0:T(8,128)(2,1)} %copy-done.6, bf16[4096,3072]{1,0:T(8,128)(2,1)} %convolution_convert_fusion.5), kind=kOutput, calls=%fused_computation.75.clone.1 | convolution fusion | flops 19453181952 | bytes 40894464 | tf_op jit(solution)/shard_map/while/body/eval_jaxpr/dot_general | solution.py:45
  397.1 30.3 %reduce-scatter.5.cloned.1.call-done = f32[96,3072]{1,0:T(8,128)} async-done(((f32[768,3072]{1,0:T(8,128)}), f32[96,3072]{1,0:T(8,128)}) %reduce-scatter.5.cloned.1.call-update) | async-done | bytes 1179664 | tf_op jit(solution)/shard_map/while/body/eval_jaxpr/reduce_scatter | solution.py:51
  429.9 68.4 %reduce-scatter.9.cloned.1.call-done = f32[384,768]{1,0:T(8,128)} async-done(((f32[3072,768]{1,0:T(8,128)}), f32[384,768]{1,0:T(8,128)}) %reduce-scatter.9.cloned.1.call-update) | async-done | bytes 1179664 | tf_op jit(solution)/shard_map/while/body/eval_jaxpr/reduce_scatter | solution.py:50
  507.6 29.4 %all-gather.21.cloned.1.call-done = bf16[1,768,3072]{2,1,0:T(8,128)(2,1)} async-done(((bf16[1,96,3072]{2,1,0:T(8,128)(2,1)}), bf16[1,768,3072]{2,1,0:T(8,128)(2,1)}) %all-gather.21.cloned.1.call-update) | async-done | bytes 4718608 | tf_op jit(solution)/shard_map/while/body/eval_jaxpr/all_gather | solution.py:32
  571.6 36.8 %bitcast_add_fusion.2 = bf16[4096,768]{1,0:T(8,128)(2,1)} fusion(bf16[4,4096,768]{2,1,0:T(8,128)(2,1)} %get-tuple-element.198, s32[]{:T(128)S(6)} %copy.11, bf16[1,3072,768]{2,1,0:T(8,128)(2,1)} %all-gather.23.cloned.1.call-done, bf16[4096,3072]{1,0:T(8,128)(2,1)} %convolution_convert_fusion.5), kind=kOutput, calls=%fused_computation.46.clone.1 | convolution fusion | flops 19459473408 | bytes 42467332 | tf_op jit(solution)/shard_map/while/body/eval_jaxpr/dot_general | solution.py:36
  608.4 27.1 %convolution_convert_fusion.6 = bf16[4096,3072]{1,0:T(8,128)(2,1)} fusion(bf16[4096,768]{1,0:T(8,128)(2,1)} %bitcast_add_fusion.2, bf16[1,768,3072]{2,1,0:T(8,128)(2,1)} %all-gather.25.cloned.1.call-done), kind=kOutput, calls=%fused_computation.39.clone.1 | convolution fusion | flops 19339935744 | bytes 36175872 | tf_op jit(solution)/shard_map/while/body/eval_jaxpr/dot_general | solution.py:34
  635.5 33.6 %fusion.142 = f32[3072,768]{1,0:T(8,128)} fusion(bf16[4096,3072]{1,0:T(8,128)(2,1)} %convolution_convert_fusion.6, bf16[4,4096,768]{2,1,0:T(8,128)(2,1)} %get-tuple-element.199, s32[]{:T(128)S(6)} %copy.11), kind=kOutput, calls=%fused_computation.36.clone.1 | convolution fusion | flops 19453181952 | bytes 40894468 | tf_op jit(solution)/shard_map/while/body/eval_jaxpr/dot_general | solution.py:45
  669.2 50.2 %fusion.137 = bf16[4096,3072]{1,0:T(8,128)(2,1)} fusion(bf16[4096,3072]{1,0:T(8,128)(2,1)} %convolution_convert_fusion.6, bf16[4,4096,768]{2,1,0:T(8,128)(2,1)} %get-tuple-element.199, s32[]{:T(128)S(6)} %copy.11, bf16[1,3072,768]{2,1,0:T(8,128)(2,1)} %all-gather.27.cloned.1.call-done), kind=kOutput, calls=%fused_computation.22.clone.2 | convolution fusion | flops 19604176896 | bytes 61341700 | tf_op jit(solution)/shard_map/while/body/eval_jaxpr/dot_general | solution.py:43
  719.4 27.4 %fusion.140 = f32[768,3072]{1,0:T(8,128)} fusion(bf16[4096,768]{1,0:T(8,128)(2,1)} %bitcast_add_fusion.2, bf16[4096,3072]{1,0:T(8,128)(2,1)} %fusion.137), kind=kOutput, calls=%fused_computation.80.clone.1 | convolution fusion | flops 19327352832 | bytes 40894464 | tf_op jit(solution)/shard_map/while/body/eval_jaxpr/dot_general | solution.py:46
  772.0 51.2 %fusion.138 = bf16[4096,3072]{1,0:T(8,128)(2,1)} fusion(bf16[4096,3072]{1,0:T(8,128)(2,1)} %convolution_convert_fusion.5, bf16[4096,768]{1,0:T(8,128)(2,1)S(1)} %add_convert_fusion.2, bf16[1,3072,768]{2,1,0:T(8,128)(2,1)} %all-gather.23.cloned.1.call-done), kind=kOutput, calls=%fused_computation.29.clone.clone.2.clone.1 | convolution fusion | flops 19604176896 | bytes 61341696 | tf_op jit(solution)/shard_map/while/body/eval_jaxpr/dot_general | solution.py:43
  823.2 27.1 %fusion.139 = f32[768,3072]{1,0:T(8,128)} fusion(bf16[4,4096,768]{2,1,0:T(8,128)(2,1)} %get-tuple-element.198, s32[]{:T(128)S(6)} %copy.11, bf16[4096,3072]{1,0:T(8,128)(2,1)} %fusion.138), kind=kOutput, calls=%fused_computation.37.clone.3 | convolution fusion | flops 19327352832 | bytes 40894468 | tf_op jit(solution)/shard_map/while/body/eval_jaxpr/dot_general | solution.py:46
  850.4 33.4 %fusion.141 = f32[3072,768]{1,0:T(8,128)} fusion(bf16[4096,768]{1,0:T(8,128)(2,1)} %copy-done.6, bf16[4096,3072]{1,0:T(8,128)(2,1)} %convolution_convert_fusion.5), kind=kOutput, calls=%fused_computation.75.clone.1 | convolution fusion | flops 19453181952 | bytes 40894464 | tf_op jit(solution)/shard_map/while/body/eval_jaxpr/dot_general | solution.py:45
  887.5 30.4 %reduce-scatter.5.cloned.1.call-done = f32[96,3072]{1,0:T(8,128)} async-done(((f32[768,3072]{1,0:T(8,128)}), f32[96,3072]{1,0:T(8,128)}) %reduce-scatter.5.cloned.1.call-update) | async-done | bytes 1179664 | tf_op jit(solution)/shard_map/while/body/eval_jaxpr/reduce_scatter | solution.py:51
  920.7 67.9 %reduce-scatter.9.cloned.1.call-done = f32[384,768]{1,0:T(8,128)} async-done(((f32[3072,768]{1,0:T(8,128)}), f32[384,768]{1,0:T(8,128)}) %reduce-scatter.9.cloned.1.call-update) | async-done | bytes 1179664 | tf_op jit(solution)/shard_map/while/body/eval_jaxpr/reduce_scatter | solution.py:50
  997.7 29.3 %all-gather.21.cloned.1.call-done = bf16[1,768,3072]{2,1,0:T(8,128)(2,1)} async-done(((bf16[1,96,3072]{2,1,0:T(8,128)(2,1)}), bf16[1,768,3072]{2,1,0:T(8,128)(2,1)}) %all-gather.21.cloned.1.call-update) | async-done | bytes 4718608 | tf_op jit(solution)/shard_map/while/body/eval_jaxpr/all_gather | solution.py:32
  1027.0 26.9 %convolution_convert_fusion.5 = bf16[4096,3072]{1,0:T(8,128)(2,1)} fusion(bf16[4,4096,768]{2,1,0:T(8,128)(2,1)} %get-tuple-element.198, s32[]{:T(128)S(6)} %copy.11, bf16[1,768,3072]{2,1,0:T(8,128)(2,1)} %all-gather.21.cloned.1.call-done), kind=kOutput, calls=%fused_computation.40.clone.1 | convolution fusion | flops 19339935744 | bytes 36175876 | tf_op jit(solution)/shard_map/while/body/eval_jaxpr/dot_general | solution.py:34
  1061.6 37.1 %bitcast_add_fusion.2 = bf16[4096,768]{1,0:T(8,128)(2,1)} fusion(bf16[4,4096,768]{2,1,0:T(8,128)(2,1)} %get-tuple-element.198, s32[]{:T(128)S(6)} %copy.11, bf16[1,3072,768]{2,1,0:T(8,128)(2,1)} %all-gather.23.cloned.1.call-done, bf16[4096,3072]{1,0:T(8,128)(2,1)} %convolution_convert_fusion.5), kind=kOutput, calls=%fused_computation.46.clone.1 | convolution fusion | flops 19459473408 | bytes 42467332 | tf_op jit(solution)/shard_map/while/body/eval_jaxpr/dot_general | solution.py:36
  1098.8 27.0 %convolution_convert_fusion.6 = bf16[4096,3072]{1,0:T(8,128)(2,1)} fusion(bf16[4096,768]{1,0:T(8,128)(2,1)} %bitcast_add_fusion.2, bf16[1,768,3072]{2,1,0:T(8,128)(2,1)} %all-gather.25.cloned.1.call-done), kind=kOutput, calls=%fused_computation.39.clone.1 | convolution fusion | flops 19339935744 | bytes 36175872 | tf_op jit(solution)/shard_map/while/body/eval_jaxpr/dot_general | solution.py:34
  1125.8 33.3 %fusion.142 = f32[3072,768]{1,0:T(8,128)} fusion(bf16[4096,3072]{1,0:T(8,128)(2,1)} %convolution_convert_fusion.6, bf16[4,4096,768]{2,1,0:T(8,128)(2,1)} %get-tuple-element.199, s32[]{:T(128)S(6)} %copy.11), kind=kOutput, calls=%fused_computation.36.clone.1 | convolution fusion | flops 19453181952 | bytes 40894468 | tf_op jit(solution)/shard_map/while/body/eval_jaxpr/dot_general | solution.py:45
  1159.2 50.2 %fusion.137 = bf16[4096,3072]{1,0:T(8,128)(2,1)} fusion(bf16[4096,3072]{1,0:T(8,128)(2,1)} %convolution_convert_fusion.6, bf16[4,4096,768]{2,1,0:T(8,128)(2,1)} %get-tuple-element.199, s32[]{:T(128)S(6)} %copy.11, bf16[1,3072,768]{2,1,0:T(8,128)(2,1)} %all-gather.27.cloned.1.call-done), kind=kOutput, calls=%fused_computation.22.clone.2 | convolution fusion | flops 19604176896 | bytes 61341700 | tf_op jit(solution)/shard_map/while/body/eval_jaxpr/dot_general | solution.py:43
  1209.4 27.1 %fusion.140 = f32[768,3072]{1,0:T(8,128)} fusion(bf16[4096,768]{1,0:T(8,128)(2,1)} %bitcast_add_fusion.2, bf16[4096,3072]{1,0:T(8,128)(2,1)} %fusion.137), kind=kOutput, calls=%fused_computation.80.clone.1 | convolution fusion | flops 19327352832 | bytes 40894464 | tf_op jit(solution)/shard_map/while/body/eval_jaxpr/dot_general | solution.py:46
  1262.1 51.1 %fusion.138 = bf16[4096,3072]{1,0:T(8,128)(2,1)} fusion(bf16[4096,3072]{1,0:T(8,128)(2,1)} %convolution_convert_fusion.5, bf16[4096,768]{1,0:T(8,128)(2,1)S(1)} %add_convert_fusion.2, bf16[1,3072,768]{2,1,0:T(8,128)(2,1)} %all-gather.23.cloned.1.call-done), kind=kOutput, calls=%fused_computation.29.clone.clone.2.clone.1 | convolution fusion | flops 19604176896 | bytes 61341696 | tf_op jit(solution)/shard_map/while/body/eval_jaxpr/dot_general | solution.py:43
  1313.3 27.4 %fusion.139 = f32[768,3072]{1,0:T(8,128)} fusion(bf16[4,4096,768]{2,1,0:T(8,128)(2,1)} %get-tuple-element.198, s32[]{:T(128)S(6)} %copy.11, bf16[4096,3072]{1,0:T(8,128)(2,1)} %fusion.138), kind=kOutput, calls=%fused_computation.37.clone.3 | convolution fusion | flops 19327352832 | bytes 40894468 | tf_op jit(solution)/shard_map/while/body/eval_jaxpr/dot_general | solution.py:46
  1340.8 33.3 %fusion.141 = f32[3072,768]{1,0:T(8,128)} fusion(bf16[4096,768]{1,0:T(8,128)(2,1)} %copy-done.6, bf16[4096,3072]{1,0:T(8,128)(2,1)} %convolution_convert_fusion.5), kind=kOutput, calls=%fused_computation.75.clone.1 | convolution fusion | flops 19453181952 | bytes 40894464 | tf_op jit(solution)/shard_map/while/body/eval_jaxpr/dot_general | solution.py:45
  1377.8 30.4 %reduce-scatter.5.cloned.1.call-done = f32[96,3072]{1,0:T(8,128)} async-done(((f32[768,3072]{1,0:T(8,128)}), f32[96,3072]{1,0:T(8,128)}) %reduce-scatter.5.cloned.1.call-update) | async-done | bytes 1179664 | tf_op jit(solution)/shard_map/while/body/eval_jaxpr/reduce_scatter | solution.py:51
  1411.1 67.9 %reduce-scatter.9.cloned.1.call-done = f32[384,768]{1,0:T(8,128)} async-done(((f32[3072,768]{1,0:T(8,128)}), f32[384,768]{1,0:T(8,128)}) %reduce-scatter.9.cloned.1.call-update) | async-done | bytes 1179664 | tf_op jit(solution)/shard_map/while/body/eval_jaxpr/reduce_scatter | solution.py:50
  1488.0 29.4 %all-gather.21.cloned.1.call-done = bf16[1,768,3072]{2,1,0:T(8,128)(2,1)} async-done(((bf16[1,96,3072]{2,1,0:T(8,128)(2,1)}), bf16[1,768,3072]{2,1,0:T(8,128)(2,1)}) %all-gather.21.cloned.1.call-update) | async-done | bytes 4718608 | tf_op jit(solution)/shard_map/while/body/eval_jaxpr/all_gather | solution.py:32
  1517.4 26.9 %convolution_convert_fusion.5 = bf16[4096,3072]{1,0:T(8,128)(2,1)} fusion(bf16[4,4096,768]{2,1,0:T(8,128)(2,1)} %get-tuple-element.198, s32[]{:T(128)S(6)} %copy.11, bf16[1,768,3072]{2,1,0:T(8,128)(2,1)} %all-gather.21.cloned.1.call-done), kind=kOutput, calls=%fused_computation.40.clone.1 | convolution fusion | flops 19339935744 | bytes 36175876 | tf_op jit(solution)/shard_map/while/body/eval_jaxpr/dot_general | solution.py:34
  1552.0 36.9 %bitcast_add_fusion.2 = bf16[4096,768]{1,0:T(8,128)(2,1)} fusion(bf16[4,4096,768]{2,1,0:T(8,128)(2,1)} %get-tuple-element.198, s32[]{:T(128)S(6)} %copy.11, bf16[1,3072,768]{2,1,0:T(8,128)(2,1)} %all-gather.23.cloned.1.call-done, bf16[4096,3072]{1,0:T(8,128)(2,1)} %convolution_convert_fusion.5), kind=kOutput, calls=%fused_computation.46.clone.1 | convolution fusion | flops 19459473408 | bytes 42467332 | tf_op jit(solution)/shard_map/while/body/eval_jaxpr/dot_general | solution.py:36
  1589.0 27.4 %convolution_convert_fusion.6 = bf16[4096,3072]{1,0:T(8,128)(2,1)} fusion(bf16[4096,768]{1,0:T(8,128)(2,1)} %bitcast_add_fusion.2, bf16[1,768,3072]{2,1,0:T(8,128)(2,1)} %all-gather.25.cloned.1.call-done), kind=kOutput, calls=%fused_computation.39.clone.1 | convolution fusion | flops 19339935744 | bytes 36175872 | tf_op jit(solution)/shard_map/while/body/eval_jaxpr/dot_general | solution.py:34
  1616.3 33.2 %fusion.142 = f32[3072,768]{1,0:T(8,128)} fusion(bf16[4096,3072]{1,0:T(8,128)(2,1)} %convolution_convert_fusion.6, bf16[4,4096,768]{2,1,0:T(8,128)(2,1)} %get-tuple-element.199, s32[]{:T(128)S(6)} %copy.11), kind=kOutput, calls=%fused_computation.36.clone.1 | convolution fusion | flops 19453181952 | bytes 40894468 | tf_op jit(solution)/shard_map/while/body/eval_jaxpr/dot_general | solution.py:45
  1649.7 50.2 %fusion.137 = bf16[4096,3072]{1,0:T(8,128)(2,1)} fusion(bf16[4096,3072]{1,0:T(8,128)(2,1)} %convolution_convert_fusion.6, bf16[4,4096,768]{2,1,0:T(8,128)(2,1)} %get-tuple-element.199, s32[]{:T(128)S(6)} %copy.11, bf16[1,3072,768]{2,1,0:T(8,128)(2,1)} %all-gather.27.cloned.1.call-done), kind=kOutput, calls=%fused_computation.22.clone.2 | convolution fusion | flops 19604176896 | bytes 61341700 | tf_op jit(solution)/shard_map/while/body/eval_jaxpr/dot_general | solution.py:43
  1699.8 27.1 %fusion.140 = f32[768,3072]{1,0:T(8,128)} fusion(bf16[4096,768]{1,0:T(8,128)(2,1)} %bitcast_add_fusion.2, bf16[4096,3072]{1,0:T(8,128)(2,1)} %fusion.137), kind=kOutput, calls=%fused_computation.80.clone.1 | convolution fusion | flops 19327352832 | bytes 40894464 | tf_op jit(solution)/shard_map/while/body/eval_jaxpr/dot_general | solution.py:46
  1752.3 51.2 %fusion.138 = bf16[4096,3072]{1,0:T(8,128)(2,1)} fusion(bf16[4096,3072]{1,0:T(8,128)(2,1)} %convolution_convert_fusion.5, bf16[4096,768]{1,0:T(8,128)(2,1)S(1)} %add_convert_fusion.2, bf16[1,3072,768]{2,1,0:T(8,128)(2,1)} %all-gather.23.cloned.1.call-done), kind=kOutput, calls=%fused_computation.29.clone.clone.2.clone.1 | convolution fusion | flops 19604176896 | bytes 61341696 | tf_op jit(solution)/shard_map/while/body/eval_jaxpr/dot_general | solution.py:43
  1803.4 27.5 %fusion.139 = f32[768,3072]{1,0:T(8,128)} fusion(bf16[4,4096,768]{2,1,0:T(8,128)(2,1)} %get-tuple-element.198, s32[]{:T(128)S(6)} %copy.11, bf16[4096,3072]{1,0:T(8,128)(2,1)} %fusion.138), kind=kOutput, calls=%fused_computation.37.clone.3 | convolution fusion | flops 19327352832 | bytes 40894468 | tf_op jit(solution)/shard_map/while/body/eval_jaxpr/dot_general | solution.py:46
  1831.1 33.3 %fusion.141 = f32[3072,768]{1,0:T(8,128)} fusion(bf16[4096,768]{1,0:T(8,128)(2,1)} %copy-done.6, bf16[4096,3072]{1,0:T(8,128)(2,1)} %convolution_convert_fusion.5), kind=kOutput, calls=%fused_computation.75.clone.1 | convolution fusion | flops 19453181952 | bytes 40894464 | tf_op jit(solution)/shard_map/while/body/eval_jaxpr/dot_general | solution.py:45
  1868.1 30.4 %reduce-scatter.5.cloned.1.call-done = f32[96,3072]{1,0:T(8,128)} async-done(((f32[768,3072]{1,0:T(8,128)}), f32[96,3072]{1,0:T(8,128)}) %reduce-scatter.5.cloned.1.call-update) | async-done | bytes 1179664 | tf_op jit(solution)/shard_map/while/body/eval_jaxpr/reduce_scatter | solution.py:51
  1901.4 68.0 %reduce-scatter.9.cloned.1.call-done = f32[384,768]{1,0:T(8,128)} async-done(((f32[3072,768]{1,0:T(8,128)}), f32[384,768]{1,0:T(8,128)}) %reduce-scatter.9.cloned.1.call-update) | async-done | bytes 1179664 | tf_op jit(solution)/shard_map/while/body/eval_jaxpr/reduce_scatter | solution.py:50
  (175 shorter events, 227.1 us)
Async XLA Ops:
  7.4 38.4 %all-gather.21.cloned.1.call-start = ((), (), s32[]{:S(2)}) async-start(), calls=%async_computation.4 | async-start | bytes 5308416 | tf_op jit(solution)/shard_map/while/body/eval_jaxpr/all_gather | solution.py:32
  9.8 70.8 %all-gather.23.cloned.1.call-start = ((), (), s32[]{:S(2)}) async-start(), calls=%async_computation.5 | async-start | bytes 5308416 | tf_op jit(solution)/shard_map/while/body/eval_jaxpr/all_gather | solution.py:33
  12.3 105.3 %all-gather.25.cloned.1.call-start = ((), (), s32[]{:S(2)}) async-start(), calls=%async_computation.6 | async-start | bytes 5308416 | tf_op jit(solution)/shard_map/while/body/eval_jaxpr/all_gather | solution.py:32
  13.0 165.3 %all-gather.27.cloned.1.call-start = ((), (), s32[]{:S(2)}) async-start(), calls=%async_computation.7 | async-start | bytes 5308416 | tf_op jit(solution)/shard_map/while/body/eval_jaxpr/all_gather | solution.py:42
  13.6 379.8 %reduce-scatter.11.cloned.1.call-start = ((), (), s32[]{:S(2)}) async-start(), calls=%async_computation.11 | async-start | bytes 10616832 | tf_op jit(solution)/shard_map/while/body/eval_jaxpr/reduce_scatter | solution.py:50
  178.3 216.7 %reduce-scatter.7.cloned.1.call-start = ((), (), s32[]{:S(2)}) async-start(), calls=%async_computation.9 | async-start | bytes 10616832 | tf_op jit(solution)/shard_map/while/body/eval_jaxpr/reduce_scatter | solution.py:51
  256.1 171.3 %reduce-scatter.5.cloned.1.call-start = ((), (), s32[]{:S(2)}) async-start(), calls=%async_computation.8 | async-start | bytes 10616832 | tf_op jit(solution)/shard_map/while/body/eval_jaxpr/reduce_scatter | solution.py:51
  281.3 51.2 %copy-start.6 = (bf16[4096,768]{1,0:T(8,128)(2,1)}, bf16[4096,768]{1,0:T(8,128)(2,1)S(1)}, u32[]{:S(2)}) copy-start(bf16[4096,768]{1,0:T(8,128)(2,1)S(1)} %add_convert_fusion.2) | copy-start | bytes 18874372 | tf_op jit(solution)/shard_map/while
  359.9 138.4 %copy-start.2 = (f32[384,768]{1,0:T(8,128)S(1)}, f32[384,768]{1,0:T(8,128)}, u32[]{:S(2)}) copy-start(f32[384,768]{1,0:T(8,128)} %get-tuple-element.185) | copy-start | bytes 3538948 | tf_op jit(solution)/shard_map/while
  359.9 138.4 %reduce-scatter.9.cloned.1.call-start = ((), (), s32[]{:S(2)}) async-start(), calls=%async_computation.10 | async-start | bytes 10616832 | tf_op jit(solution)/shard_map/while/body/eval_jaxpr/reduce_scatter | solution.py:50
  395.0 104.9 %copy-start.1 = (f32[384,768]{1,0:T(8,128)}, f32[384,768]{1,0:T(8,128)S(1)}, u32[]{:S(2)}) copy-start(f32[384,768]{1,0:T(8,128)S(1)} %select_add_fusion.11) | copy-start | bytes 3538948 | tf_op jit(solution)/shard_map/while
  397.1 102.8 %copy-start.5 = (f32[96,3072]{1,0:T(8,128)}, f32[96,3072]{1,0:T(8,128)S(1)}, u32[]{:S(2)}) copy-start(f32[96,3072]{1,0:T(8,128)S(1)} %select_add_fusion.9) | copy-start | bytes 3538948 | tf_op jit(solution)/shard_map/while
  501.4 35.6 %all-gather.21.cloned.1.call-start = ((), (), s32[]{:S(2)}) async-start(), calls=%async_computation.4 | async-start | bytes 5308416 | tf_op jit(solution)/shard_map/while/body/eval_jaxpr/all_gather | solution.py:32
  503.8 67.8 %all-gather.23.cloned.1.call-start = ((), (), s32[]{:S(2)}) async-start(), calls=%async_computation.5 | async-start | bytes 5308416 | tf_op jit(solution)/shard_map/while/body/eval_jaxpr/all_gather | solution.py:33
  506.2 102.2 %all-gather.25.cloned.1.call-start = ((), (), s32[]{:S(2)}) async-start(), calls=%async_computation.6 | async-start | bytes 5308416 | tf_op jit(solution)/shard_map/while/body/eval_jaxpr/all_gather | solution.py:32
  507.0 162.2 %all-gather.27.cloned.1.call-start = ((), (), s32[]{:S(2)}) async-start(), calls=%async_computation.7 | async-start | bytes 5308416 | tf_op jit(solution)/shard_map/while/body/eval_jaxpr/all_gather | solution.py:42
  507.6 376.3 %reduce-scatter.11.cloned.1.call-start = ((), (), s32[]{:S(2)}) async-start(), calls=%async_computation.11 | async-start | bytes 10616832 | tf_op jit(solution)/shard_map/while/body/eval_jaxpr/reduce_scatter | solution.py:50
  669.1 216.3 %reduce-scatter.7.cloned.1.call-start = ((), (), s32[]{:S(2)}) async-start(), calls=%async_computation.9 | async-start | bytes 10616832 | tf_op jit(solution)/shard_map/while/body/eval_jaxpr/reduce_scatter | solution.py:51
  746.8 171.1 %reduce-scatter.5.cloned.1.call-start = ((), (), s32[]{:S(2)}) async-start(), calls=%async_computation.8 | async-start | bytes 10616832 | tf_op jit(solution)/shard_map/while/body/eval_jaxpr/reduce_scatter | solution.py:51
  772.0 51.2 %copy-start.6 = (bf16[4096,768]{1,0:T(8,128)(2,1)}, bf16[4096,768]{1,0:T(8,128)(2,1)S(1)}, u32[]{:S(2)}) copy-start(bf16[4096,768]{1,0:T(8,128)(2,1)S(1)} %add_convert_fusion.2) | copy-start | bytes 18874372 | tf_op jit(solution)/shard_map/while
  850.3 138.3 %copy-start.2 = (f32[384,768]{1,0:T(8,128)S(1)}, f32[384,768]{1,0:T(8,128)}, u32[]{:S(2)}) copy-start(f32[384,768]{1,0:T(8,128)} %get-tuple-element.185) | copy-start | bytes 3538948 | tf_op jit(solution)/shard_map/while
  850.4 138.2 %reduce-scatter.9.cloned.1.call-start = ((), (), s32[]{:S(2)}) async-start(), calls=%async_computation.10 | async-start | bytes 10616832 | tf_op jit(solution)/shard_map/while/body/eval_jaxpr/reduce_scatter | solution.py:50
  885.4 104.8 %copy-start.1 = (f32[384,768]{1,0:T(8,128)}, f32[384,768]{1,0:T(8,128)S(1)}, u32[]{:S(2)}) copy-start(f32[384,768]{1,0:T(8,128)S(1)} %select_add_fusion.11) | copy-start | bytes 3538948 | tf_op jit(solution)/shard_map/while
  887.5 102.7 %copy-start.5 = (f32[96,3072]{1,0:T(8,128)}, f32[96,3072]{1,0:T(8,128)S(1)}, u32[]{:S(2)}) copy-start(f32[96,3072]{1,0:T(8,128)S(1)} %select_add_fusion.9) | copy-start | bytes 3538948 | tf_op jit(solution)/shard_map/while
  991.5 35.5 %all-gather.21.cloned.1.call-start = ((), (), s32[]{:S(2)}) async-start(), calls=%async_computation.4 | async-start | bytes 5308416 | tf_op jit(solution)/shard_map/while/body/eval_jaxpr/all_gather | solution.py:32
  993.9 67.8 %all-gather.23.cloned.1.call-start = ((), (), s32[]{:S(2)}) async-start(), calls=%async_computation.5 | async-start | bytes 5308416 | tf_op jit(solution)/shard_map/while/body/eval_jaxpr/all_gather | solution.py:33
  996.3 102.4 %all-gather.25.cloned.1.call-start = ((), (), s32[]{:S(2)}) async-start(), calls=%async_computation.6 | async-start | bytes 5308416 | tf_op jit(solution)/shard_map/while/body/eval_jaxpr/all_gather | solution.py:32
  997.1 162.1 %all-gather.27.cloned.1.call-start = ((), (), s32[]{:S(2)}) async-start(), calls=%async_computation.7 | async-start | bytes 5308416 | tf_op jit(solution)/shard_map/while/body/eval_jaxpr/all_gather | solution.py:42
  997.7 376.5 %reduce-scatter.11.cloned.1.call-start = ((), (), s32[]{:S(2)}) async-start(), calls=%async_computation.11 | async-start | bytes 10616832 | tf_op jit(solution)/shard_map/while/body/eval_jaxpr/reduce_scatter | solution.py:50
  1159.2 216.6 %reduce-scatter.7.cloned.1.call-start = ((), (), s32[]{:S(2)}) async-start(), calls=%async_computation.9 | async-start | bytes 10616832 | tf_op jit(solution)/shard_map/while/body/eval_jaxpr/reduce_scatter | solution.py:51
  1236.6 171.6 %reduce-scatter.5.cloned.1.call-start = ((), (), s32[]{:S(2)}) async-start(), calls=%async_computation.8 | async-start | bytes 10616832 | tf_op jit(solution)/shard_map/while/body/eval_jaxpr/reduce_scatter | solution.py:51
  1262.1 51.2 %copy-start.6 = (bf16[4096,768]{1,0:T(8,128)(2,1)}, bf16[4096,768]{1,0:T(8,128)(2,1)S(1)}, u32[]{:S(2)}) copy-start(bf16[4096,768]{1,0:T(8,128)(2,1)S(1)} %add_convert_fusion.2) | copy-start | bytes 18874372 | tf_op jit(solution)/shard_map/while
  1340.7 138.3 %copy-start.2 = (f32[384,768]{1,0:T(8,128)S(1)}, f32[384,768]{1,0:T(8,128)}, u32[]{:S(2)}) copy-start(f32[384,768]{1,0:T(8,128)} %get-tuple-element.185) | copy-start | bytes 3538948 | tf_op jit(solution)/shard_map/while
  1340.7 138.2 %reduce-scatter.9.cloned.1.call-start = ((), (), s32[]{:S(2)}) async-start(), calls=%async_computation.10 | async-start | bytes 10616832 | tf_op jit(solution)/shard_map/while/body/eval_jaxpr/reduce_scatter | solution.py:50
  1375.7 104.8 %copy-start.1 = (f32[384,768]{1,0:T(8,128)}, f32[384,768]{1,0:T(8,128)S(1)}, u32[]{:S(2)}) copy-start(f32[384,768]{1,0:T(8,128)S(1)} %select_add_fusion.11) | copy-start | bytes 3538948 | tf_op jit(solution)/shard_map/while
  1377.8 102.7 %copy-start.5 = (f32[96,3072]{1,0:T(8,128)}, f32[96,3072]{1,0:T(8,128)S(1)}, u32[]{:S(2)}) copy-start(f32[96,3072]{1,0:T(8,128)S(1)} %select_add_fusion.9) | copy-start | bytes 3538948 | tf_op jit(solution)/shard_map/while
  1481.8 35.6 %all-gather.21.cloned.1.call-start = ((), (), s32[]{:S(2)}) async-start(), calls=%async_computation.4 | async-start | bytes 5308416 | tf_op jit(solution)/shard_map/while/body/eval_jaxpr/all_gather | solution.py:32
  1484.2 67.8 %all-gather.23.cloned.1.call-start = ((), (), s32[]{:S(2)}) async-start(), calls=%async_computation.5 | async-start | bytes 5308416 | tf_op jit(solution)/shard_map/while/body/eval_jaxpr/all_gather | solution.py:33
  1486.6 102.3 %all-gather.25.cloned.1.call-start = ((), (), s32[]{:S(2)}) async-start(), calls=%async_computation.6 | async-start | bytes 5308416 | tf_op jit(solution)/shard_map/while/body/eval_jaxpr/all_gather | solution.py:32
  1487.2 162.4 %all-gather.27.cloned.1.call-start = ((), (), s32[]{:S(2)}) async-start(), calls=%async_computation.7 | async-start | bytes 5308416 | tf_op jit(solution)/shard_map/while/body/eval_jaxpr/all_gather | solution.py:42
  1488.0 376.4 %reduce-scatter.11.cloned.1.call-start = ((), (), s32[]{:S(2)}) async-start(), calls=%async_computation.11 | async-start | bytes 10616832 | tf_op jit(solution)/shard_map/while/body/eval_jaxpr/reduce_scatter | solution.py:50
  1649.6 216.4 %reduce-scatter.7.cloned.1.call-start = ((), (), s32[]{:S(2)}) async-start(), calls=%async_computation.9 | async-start | bytes 10616832 | tf_op jit(solution)/shard_map/while/body/eval_jaxpr/reduce_scatter | solution.py:51
  1727.0 171.6 %reduce-scatter.5.cloned.1.call-start = ((), (), s32[]{:S(2)}) async-start(), calls=%async_computation.8 | async-start | bytes 10616832 | tf_op jit(solution)/shard_map/while/body/eval_jaxpr/reduce_scatter | solution.py:51
  1752.3 51.2 %copy-start.6 = (bf16[4096,768]{1,0:T(8,128)(2,1)}, bf16[4096,768]{1,0:T(8,128)(2,1)S(1)}, u32[]{:S(2)}) copy-start(bf16[4096,768]{1,0:T(8,128)(2,1)S(1)} %add_convert_fusion.2) | copy-start | bytes 18874372 | tf_op jit(solution)/shard_map/while
  1831.0 138.4 %copy-start.2 = (f32[384,768]{1,0:T(8,128)S(1)}, f32[384,768]{1,0:T(8,128)}, u32[]{:S(2)}) copy-start(f32[384,768]{1,0:T(8,128)} %get-tuple-element.185) | copy-start | bytes 3538948 | tf_op jit(solution)/shard_map/while
  1831.0 138.4 %reduce-scatter.9.cloned.1.call-start = ((), (), s32[]{:S(2)}) async-start(), calls=%async_computation.10 | async-start | bytes 10616832 | tf_op jit(solution)/shard_map/while/body/eval_jaxpr/reduce_scatter | solution.py:50
  1866.0 105.0 %copy-start.1 = (f32[384,768]{1,0:T(8,128)}, f32[384,768]{1,0:T(8,128)S(1)}, u32[]{:S(2)}) copy-start(f32[384,768]{1,0:T(8,128)S(1)} %select_add_fusion.11) | copy-start | bytes 3538948 | tf_op jit(solution)/shard_map/while
  1868.1 102.9 %copy-start.5 = (f32[96,3072]{1,0:T(8,128)}, f32[96,3072]{1,0:T(8,128)S(1)}, u32[]{:S(2)}) copy-start(f32[96,3072]{1,0:T(8,128)S(1)} %select_add_fusion.9) | copy-start | bytes 3538948 | tf_op jit(solution)/shard_map/while
  (12 other events, 278.4 us)
Sparse Core Ops, SparseCore 0:
  10.1 35.7 all-gather.20
  47.7 32.9 all-gather.22
  83.0 32.9 all-gather.24
  117.7 32.9 all-gather.26
  178.4 67.3 reduce-scatter.10
  256.2 67.3 reduce-scatter.6
  360.0 67.3 reduce-scatter.4
  430.8 67.4 reduce-scatter.8
  504.0 32.9 all-gather.20
  538.7 32.9 all-gather.22
  574.0 32.9 all-gather.24
  608.7 32.9 all-gather.26
  669.2 67.3 reduce-scatter.10
  746.9 67.3 reduce-scatter.6
  850.4 67.4 reduce-scatter.4
  921.2 67.3 reduce-scatter.8
  994.0 32.9 all-gather.20
  1028.7 32.9 all-gather.22
  1064.0 32.9 all-gather.24
  1098.6 32.9 all-gather.26
  1159.3 67.3 reduce-scatter.10
  1236.7 67.3 reduce-scatter.6
  1340.8 67.3 reduce-scatter.4
  1411.5 67.4 reduce-scatter.8
  1484.4 32.9 all-gather.20
  1519.1 32.9 all-gather.22
  1554.3 32.9 all-gather.24
  1589.1 32.9 all-gather.26
  1649.7 67.4 reduce-scatter.10
  1727.1 67.4 reduce-scatter.6
  1831.1 67.4 reduce-scatter.4
  1902.0 67.4 reduce-scatter.8
where the time goes:
time: 1990 us
  matrix products  1360 us (68%)
  waiting for transfers between devices  551 us (28%)
  other arithmetic  38.3 us (2%)
  local copies, waits for them, and re-layouts  22.9 us (1%)
    dot_general x8, matrix products, micro_body(): lax.dot_general(grad_x, w_out_full, contract_cols, preferred_element_type...  406 us
    reduce_scatter x8, waiting for transfers between devices, micro_body(): lax.psum_scatter(part_out, GROUP_AXIS, scatter_dimension=0, tiled=True)  272 us
    dot_general x8, matrix products, micro_body(): lax.dot_general(active, grad_x, contract_rows, preferred_element_type=jnp...  267 us
    dot_general x8, matrix products, micro_body(): lax.dot_general(x_saved, grad_hid, contract_rows, preferred_element_type=...  218 us
    dot_general x8, matrix products, micro_body(): jnp.dot(x_cur, w_in_full, preferred_element_type=jnp.float32)  216 us
    dot_general x4, matrix products, micro_body(): jnp.dot(gelu_pair(hidden)[0], w_out_full, preferred_element_type=jnp.floa...  148 us
    reduce_scatter x8, waiting for transfers between devices, micro_body(): lax.psum_scatter(part_in, GROUP_AXIS, scatter_dimension=0, tiled=True)  122 us
    all_gather x8, waiting for transfers between devices, micro_body(): lax.all_gather(w_in_loc[layer_idx], GROUP_AXIS, axis=0, tiled=True)  120 us
  transfers between devices with their start and end apart: 32, of which 16 were waited for; matrix products, arithmetic and copies ran while one was open for 70% of the time, Pallas kernels for 0%

commit v1 on v0

v1 whole, which is shorter than its diff:
```python
import functools
import math
import jax
import jax.numpy as jnp
from jax import lax
from jax.experimental import pallas as pl
from jax.experimental.layout import Layout, with_layout_constraint
from jax.experimental.pallas import tpu as pltpu
from jax.sharding import PartitionSpec as P

GROUP_AXIS = "fsdp"
BF, F32 = jnp.bfloat16, jnp.float32
C0 = math.sqrt(2.0 / math.pi)
C1 = C0 * 0.044715
VMEM_LIMIT = 67043328
ROW_BLOCK = 64


def dot(a, b):
    return jnp.dot(a, b, preferred_element_type=F32)


def dot_bt(a, b):
    return lax.dot_general(a, b, (((1,), (1,)), ((), ())), preferred_element_type=F32)


def gelu_value(hidden):
    u = hidden.astype(F32)
    t = jnp.tanh(u * (C1 * (u * u) + C0))
    return (0.5 * u * (1.0 + t)).astype(BF)


def gelu_pair(hidden):
    u = hidden.astype(F32)
    m = u * u
    t = jnp.tanh(u * (C1 * m + C0))
    s = 0.5 + 0.5 * t
    a = u * s
    slope = s + a * ((1.0 - t) * (3.0 * C1 * m + C0))
    return a.astype(BF), slope


def rows_of(width, tile):
    return pl.BlockSpec((tile, width), lambda i: (i, 0))


def resident(shape):
    return pl.BlockSpec(shape, lambda i: (0,) * len(shape), pipeline_mode=pl.Buffered(1))


def call(kernel, name, macs, **kw):
    return pl.pallas_call(
        kernel,
        name=name,
        compiler_params=pltpu.CompilerParams(vmem_limit_bytes=VMEM_LIMIT, dimension_semantics=("arbitrary",)),
        cost_estimate=pl.CostEstimate(flops=2 * macs, bytes_accessed=1 << 20, transcendentals=0),
        **kw,
    )


def hidden_kernel(x_ref, w_ref, h_ref):
    h_ref[...] = dot(x_ref[...], w_ref[...]).astype(BF)


def hidden_of(x, w, tile):
    tokens, width = x.shape
    hid = w.shape[1]
    return call(
        hidden_kernel, "hidden", tokens * width * hid,
        grid=(tokens // tile,),
        in_specs=[rows_of(width, tile), resident(w.shape)],
        out_specs=rows_of(hid, tile),
        out_shape=jax.ShapeDtypeStruct((tokens, hid), BF),
    )(x, w)


def part_rows(w_ref, lo, up, start, block):
    wide = up - lo
    pieces = []
    while block:
        owner, skip = divmod(start, wide)
        take = min(wide - skip, block)
        pieces.append(w_ref[owner, pl.ds(lo + skip, take), :])
        start, block = start + take, block - take
    return pieces[0] if len(pieces) == 1 else jnp.concatenate(pieces, 0)


def residual_kernel(tile, block, parts, x_ref, h_ref, w_ref, y_ref, total_scr):
    owners = w_ref.shape[0]
    base = 0
    for lo, up in parts:
        hid = owners * (up - lo)
        for c in range(hid // block):
            cols = pl.ds(base + c * block, block)
            active = jnp.concatenate(
                [gelu_value(h_ref[pl.ds(r * ROW_BLOCK, ROW_BLOCK), cols]) for r in range(tile // ROW_BLOCK)], 0)
            part = dot(active, part_rows(w_ref, lo, up, c * block, block))
            if base + c == 0:
                total_scr[...] = part
            else:
                total_scr[...] += part
        base += hid
    y_ref[...] = x_ref[...] + total_scr[...].astype(BF)


def residual_of(x, h, w, parts, tile, block):
    tokens, width = x.shape
    hid = h.shape[1]
    return call(
        functools.partial(residual_kernel, tile, block, parts), "residual", tokens * width * hid,
        grid=(tokens // tile,),
        in_specs=[rows_of(width, tile), rows_of(hid, tile), resident(w.shape)],
        out_specs=rows_of(width, tile),
        out_shape=jax.ShapeDtypeStruct(x.shape, BF),
        scratch_shapes=[pltpu.VMEM((tile, width), F32)],
    )(x, h, w)


def row_blocks(value):
    return [value[r:r + ROW_BLOCK] for r in range(0, value.shape[0], ROW_BLOCK)]


def hidden_grads(h_blocks, da, cols, dh_scr):
    actives, grads = [], []
    for r, (h, da_rows) in enumerate(zip(h_blocks, row_blocks(da))):
        active, slope = gelu_pair(h)
        grad = (da_rows.astype(F32) * slope).astype(BF)
        if dh_scr is not None:
            dh_scr[pl.ds(r * ROW_BLOCK, ROW_BLOCK), cols] = grad
        actives.append(active)
        grads.append(grad)
    return jnp.concatenate(actives, 0), jnp.concatenate(grads, 0)


def add_grads(active, grad, x_t, e_t, cols, g_in_acc, g_out_acc):
    g_out_acc[:, cols] += dot(e_t, active)
    grad_in = dot(x_t, grad)
    g_in_acc[:, :, cols] += grad_in.reshape(g_in_acc.shape[0], g_in_acc.shape[1], grad_in.shape[1])


def pipelined(n, first, second):
    ready = first(0)
    for c in range(n):
        following = first(c + 1) if c + 1 < n else None
        second(c, ready)
        ready = following


def clear(*accs):
    @pl.when(pl.program_id(0) == 0)
    def _():
        for acc in accs:
            acc[...] = jnp.zeros_like(acc)


def flush(g_in_acc, g_out_acc, grads_out, sems):
    owners, rows, hid = g_in_acc.shape
    own = hid // owners

    @pl.when(pl.program_id(0) == pl.num_programs(0) - 1)
    def _():
        copies = []
        for d in range(owners):
            cols = pl.ds(d * own, own)
            copies.append(pltpu.make_async_copy(g_out_acc.at[:, cols], grads_out.at[d, 0], sems.at[d]))
            copies.append(pltpu.make_async_copy(
                g_in_acc.at[:, :, cols], grads_out.at[:, 1, pl.ds(d * rows, rows), :], sems.at[owners + d]))
        for copy in copies:
            copy.start()
        for copy in copies:
            copy.wait()


def grad_shapes(width, hid, owners):
    out = jax.ShapeDtypeStruct((owners, 2, width, hid // owners), F32)
    scratch = [
        pltpu.VMEM((owners, width // owners, hid), F32),
        pltpu.VMEM((width, hid), F32),
        pltpu.SemaphoreType.DMA((2 * owners,)),
    ]
    return out, scratch


def top_kernel(tile, block, x_ref, e_ref, w1_ref, w2_ref, e_out, grads_out, g_in_acc, g_out_acc, sems, dh_scr):
    clear(g_in_acc, g_out_acc)
    x, e = x_ref[...], e_ref[...]
    x_t, e_t = x.T, e.T

    def first(c):
        cols = pl.ds(c * block, block)
        h = dot(x, w1_ref[:, cols]).astype(BF)
        da = dot_bt(e, w2_ref[cols, :]).astype(BF)
        return hidden_grads(row_blocks(h), da, cols, dh_scr)

    def second(c, ready):
        add_grads(*ready, x_t, e_t, pl.ds(c * block, block), g_in_acc, g_out_acc)

    pipelined(w1_ref.shape[1] // block, first, second)
    e_out[...] = (e.astype(F32) + dot_bt(dh_scr[...], w1_ref[...])).astype(BF)
    flush(g_in_acc, g_out_acc, grads_out, sems)


def top_layer(x, e, w1, w2, owners, tile, block):
    tokens, width = x.shape
    hid = w1.shape[1]
    out, scratch = grad_shapes(width, hid, owners)
    return call(
        functools.partial(top_kernel, tile, block), "top_layer", 5 * tokens * width * hid,
        grid=(tokens // tile,),
        in_specs=[rows_of(width, tile), rows_of(width, tile), resident(w1.shape), resident(w2.shape)],
        out_specs=[rows_of(width, tile), pl.BlockSpec(memory_space=pl.ANY)],
        out_shape=[jax.ShapeDtypeStruct(x.shape, BF), out],
        scratch_shapes=scratch + [pltpu.VMEM((tile, hid), BF)],
        input_output_aliases={0: 0},
    )(x, e, w1, w2)


def bottom_kernel(tile, block, part, x_ref, e_ref, h_ref, w2_ref, grads_out, g_in_acc, g_out_acc, sems):
    clear(g_in_acc, g_out_acc)
    e = e_ref[...]
    x_t, e_t = x_ref[...].T, e.T

    def first(c):
        cols = pl.ds(c * block, block)
        da = dot_bt(e, part_rows(w2_ref, *part, c * block, block)).astype(BF)
        h_blocks = [h_ref[pl.ds(r, ROW_BLOCK), cols] for r in range(0, tile, ROW_BLOCK)]
        return hidden_grads(h_blocks, da, cols, None)

    def second(c, ready):
        add_grads(*ready, x_t, e_t, pl.ds(c * block, block), g_in_acc, g_out_acc)

    pipelined(h_ref.shape[1] // block, first, second)
    flush(g_in_acc, g_out_acc, grads_out, sems)


def bottom_part(x, e, h, w2, part, first, tile, block):
    tokens, width = x.shape
    owners = w2.shape[0]
    hid = owners * (part[1] - part[0])
    out, scratch = grad_shapes(width, hid, owners)
    return call(
        functools.partial(bottom_kernel, tile, block, part), "bottom_part", 3 * tokens * width * hid,
        grid=(tokens // tile,),
        in_specs=[rows_of(width, tile), rows_of(width, tile), pl.BlockSpec((tile, hid), lambda i: (i, first // hid)), resident(w2.shape)],
        out_specs=pl.BlockSpec(memory_space=pl.ANY),
        out_shape=out,
        scratch_shapes=scratch,
    )(x, e, h, w2)


def part_columns_kernel(parts, owners, w_ref, out_ref):
    own = w_ref.shape[2] // owners
    base = 0
    for lo, up in parts:
        for d in range(owners):
            out_ref[:, pl.ds(base, up - lo)] = w_ref[0, :, pl.ds(d * own + lo, up - lo)]
            base += up - lo


def part_columns(w, parts, owners):
    _, rows, hid = w.shape
    return call(
        functools.partial(part_columns_kernel, parts, owners), "part_columns", rows * hid,
        grid=(1,),
        in_specs=[pl.BlockSpec((1, rows, hid), lambda i: (0, 0, 0))],
        out_specs=resident((rows, hid)),
        out_shape=jax.ShapeDtypeStruct((rows, hid), w.dtype),
    )(w)


def assemble_kernel(places, *refs):
    g_in, g_out = refs[-2:]
    _, rows, _ = g_in.shape
    _, own, width = g_out.shape
    for (layer, lo, up), ref in zip(places, refs):
        g_out[layer, pl.ds(lo, up - lo), :] = ref[pl.ds(0, width), :].T
        for d in range(width // rows):
            g_in[layer, :, pl.ds(d * own + lo, up - lo)] = ref[pl.ds(width + d * rows, rows), :]


def assemble(places, sums, rows, hid, own, width):
    shapes = ((2, rows, hid), (2, own, width))
    return call(
        functools.partial(assemble_kernel, places), "assemble", rows * hid,
        grid=(1,),
        in_specs=[resident(a.shape) for a in sums],
        out_specs=[resident(shape) for shape in shapes],
        out_shape=[jax.ShapeDtypeStruct(shape, F32) for shape in shapes],
    )(*sums)


def gather(rows):
    return lax.all_gather(rows, GROUP_AXIS, axis=0, tiled=True)


def scatter_sum(grads):
    total = lax.psum_scatter(grads.reshape(-1, grads.shape[-1]), GROUP_AXIS, scatter_dimension=0, tiled=True)
    return with_layout_constraint(total, Layout(major_to_minor=(0, 1)))


def solution(mesh):
    row_spec = P(None, GROUP_AXIS, None)
    owners = mesh.shape[GROUP_AXIS]

    def local_run(acts_loc, cot_loc, w_in_loc, w_out_loc):
        micro, tokens_loc, width = acts_loc.shape
        hid = w_in_loc.shape[2]
        rows, own = width // owners, hid // owners
        tokens = micro * tokens_loc
        x0 = acts_loc.reshape(tokens, width)
        e2 = cot_loc.reshape(tokens, width)

        parts = ((0, own - 128), (own - 128, own))
        w1 = gather(part_columns(w_in_loc, parts, owners))
        w1, first_out = lax.optimization_barrier((w1, w_out_loc[0]))
        w2 = gather(first_out)
        h0 = hidden_of(x0, w1, 1024)
        later_in, later_out, h0 = lax.optimization_barrier((w_in_loc[1], w_out_loc[1], h0))
        w1_top, w2_top = gather(later_in), gather(later_out)
        w2 = w2.reshape(owners, own, width)
        x1 = residual_of(x0, h0, w2, parts, 512, 1024)
        e1, top = top_layer(x1, e2, w1_top, w2_top, owners, 512, 1024)
        top = scatter_sum(top)
        large = scatter_sum(bottom_part(x0, e1, h0, w2, parts[0], 0, 1024, 512))
        e1, top = lax.optimization_barrier((e1, top))
        small = scatter_sum(bottom_part(x0, e1, h0, w2, parts[1], hid - owners * 128, 1024, 256))
        places = ((1, 0, own), (0, *parts[0]), (0, *parts[1]))
        return assemble(places, (top, large, small), rows, hid, own, width)

    return jax.shard_map(local_run, mesh=mesh, in_specs=(row_spec, row_spec, row_spec, row_spec), out_specs=(row_spec, row_spec), check_vma=False)
```

time: 1990 us -> 1010 us (0.51)
  matrix products: 1360 us -> 0 us
  Pallas kernels: 0 us -> 900 us
  waiting for transfers between devices: 551 us -> 88.2 us
  other arithmetic: 38.3 us -> 0 us
    dot_general x40 -> x0, matrix products: 1360 us -> none  [the longest x8 406 us: micro_body(): lax.dot_general(grad_x, w_out_full, contract_cols, preferred_element_type...]
    pallas_call x0 -> x7, Pallas kernels: none -> 900 us  [the longest x1 422 us: top_layer(): call(functools.partial(top_kernel, tile, block), 'top_layer', 5 * tokens...]
    reduce_scatter x16 -> x3, waiting for transfers between devices: 394 us -> 52.9 us  [scatter_sum(): lax.psum_scatter(grads.reshape(-1, grads.shape[-1]), GROUP_AXIS, scatter_...]
    all_gather x16 -> x4, waiting for transfers between devices: 152 us -> 34.6 us  [gather(): return lax.all_gather(rows, GROUP_AXIS, axis=0, tiled=True)]
    add x16 -> x0, other arithmetic: 31.9 us -> none  [the longest x8 19.3 us: micro_body(): acc_in[layer_idx]]
  transfers between devices with their start and end apart: 32 -> 7, of which waited for: 16 -> 2; matrix products, arithmetic and copies ran while one was open for 70% -> 0% of each run, Pallas kernels for 0% -> 47%
where the time goes in v1:
time: 1010 us
  Pallas kernels  900 us (89%)
  waiting for transfers between devices  88.2 us (9%)
  between operations  14.2 us (1%)
    pallas_call x1, Pallas kernels, top_layer(): call(functools.partial(top_kernel, tile, block), 'top_layer', 5 * tokens...  422 us
    pallas_call x2, Pallas kernels, bottom_part(): call(functools.partial(bottom_kernel, tile, block, part), 'bottom_part',...  279 us
    pallas_call x1, Pallas kernels, residual_of(): call(functools.partial(residual_kernel, tile, block, parts), 'residual',...  105 us
    pallas_call x1, Pallas kernels, hidden_of(): call(hidden_kernel, 'hidden', tokens * width * hid, grid=(tokens // tile,...  86.5 us
    reduce_scatter x3, waiting for transfers between devices, scatter_sum(): lax.psum_scatter(grads.reshape(-1, grads.shape[-1]), GROUP_AXIS, scatter_...  52.9 us
    all_gather x4, waiting for transfers between devices, gather(): return lax.all_gather(rows, GROUP_AXIS, axis=0, tiled=True)  34.6 us
  transfers between devices with their start and end apart: 7, of which 2 were waited for; matrix products, arithmetic and copies ran while one was open for 0% of the time, Pallas kernels for 47%

profile of v1, /device:TPU:0, one launch (start us, length us, event | category | flops | bytes accessed | tf_op | source)
XLA Modules:
  0.0 1006.8 jit_solution(1947536944091956413)
XLA Ops:
  7.2 0.0 all-gather.5.cloned.1.call-start
  7.2 1.9 part_columns.1
  9.2 0.0 all-gather.5.cloned.1.call-update
  9.2 0.0 all-gather.7.cloned.1.call-start
  9.2 2.3 slice_bitcast_fusion
  11.6 34.6 %all-gather.5.cloned.1.call-done.w_ref = bf16[768,3072]{1,0:T(8,128)(2,1)} async-done(((bf16[96,3072]{1,0:T(8,128)(2,1)}), bf16[768,3072]{1,0:T(8,128)(2,1)}) %all-gather.5.cloned.1.call-update) | async-done | bytes 4718608 | tf_op jit(solution)/shard_map/all_gather | solution.py:293
  46.2 0.0 all-gather.7.cloned.1.call-update
  46.2 0.0 all-gather.9.cloned.1.call-start
  46.2 1.9 slice_bitcast_fusion.2
  48.2 86.5 %hidden.1.h_ref = bf16[16384,3072]{1,0:T(8,128)(2,1)} custom-call(bf16[16384,768]{1,0:T(8,128)(2,1)} %bitcast.16, bf16[768,3072]{1,0:T(8,128)(2,1)} %all-gather.5.cloned.1.call-done.w_ref), custom_call_target="tpu_custom_call" | custom-call | flops 77309411328 | bytes 1048576 | tf_op jit(solution)/shard_map/hidden/pallas_call | solution.py:68
  134.6 0.0 all-gather.9.cloned.1.call-update
  134.7 0.0 all-gather.11.cloned.1.call-start
  134.7 0.5 all-gather.11.cloned.1.call-update
  135.2 0.0 reduce-scatter.4.cloned.1.call-start
  135.3 0.0 all-gather.7.cloned.1.call-done
  135.3 105.5 %residual.1.x_ref = bf16[16384,768]{1,0:T(8,128)(2,1)} custom-call(bf16[16384,768]{1,0:T(8,128)(2,1)} %bitcast.17, bf16[16384,3072]{1,0:T(8,128)(2,1)} %hidden.1.h_ref, bf16[8,384,768]{2,1,0:T(8,128)(2,1)} %bitcast.20), custom_call_target="tpu_custom_call" | custom-call | flops 77309411328 | bytes 1048576 | tf_op jit(solution)/shard_map/residual/pallas_call | solution.py:109
  240.8 0.0 all-gather.9.cloned.1.call-done.w1_ref
  240.8 0.0 all-gather.11.cloned.1.call-done.w2_ref
  240.8 422.2 %top_layer.1 = (bf16[16384,768]{1,0:T(8,128)(2,1)}, f32[8,2,768,384]{3,2,1,0:T(8,128)}) custom-call(bf16[16384,768]{1,0:T(8,128)(2,1)} %residual.1.x_ref, bf16[16384,768]{1,0:T(8,128)(2,1)} %bitcast.15, bf16[768,3072]{1,0:T(8,128)(2,1)} %all-gather.9.cloned.1.call-done.w1_ref, ...), custom_call_target="tpu_custom_call", output_to_operand_aliasing={{0}: (0, {})} | custom-call | flops 386547056640 | bytes 1048576 | tf_op jit(solution)/shard_map/top_layer/pallas_call | solution.py:207
  663.0 0.0 reduce-scatter.4.cloned.1.call-update
  663.0 0.0 reduce-scatter.6.cloned.1.call-start
  663.1 183.0 %bottom_part.2 = f32[8,2,768,256]{3,2,1,0:T(8,128)} custom-call(bf16[16384,768]{1,0:T(8,128)(2,1)} %bitcast.18, bf16[16384,768]{1,0:T(8,128)(2,1)} %get-tuple-element.19.e_ref, bf16[16384,3072]{1,0:T(8,128)(2,1)} %hidden.1.h_ref, bf16[8,384,768]{2,1,0:T(8,128)(2,1)} %bitcast.21), custom_call_target="tpu_custom_call" | custom-call | flops 154618822656 | bytes 1048576 | tf_op jit(solution)/shard_map/bottom_part/pallas_call | solution.py:241
  846.1 0.0 reduce-scatter.6.cloned.1.call-update
  846.2 0.0 reduce-scatter.8.cloned.1.call-start
  846.2 0.0 reduce-scatter.4.cloned.1.call-done.refs_0_
  846.2 95.5 %bottom_part.3 = f32[8,2,768,128]{3,2,1,0:T(8,128)} custom-call(bf16[16384,768]{1,0:T(8,128)(2,1)} %bitcast.19, bf16[16384,768]{1,0:T(8,128)(2,1)} %get-tuple-element.19.e_ref, bf16[16384,3072]{1,0:T(8,128)(2,1)} %hidden.1.h_ref, bf16[8,384,768]{2,1,0:T(8,128)(2,1)} %bitcast.22), custom_call_target="tpu_custom_call" | custom-call | flops 77309411328 | bytes 1048576 | tf_op jit(solution)/shard_map/bottom_part/pallas_call | solution.py:241
  941.8 0.0 reduce-scatter.8.cloned.1.call-update
  941.8 0.0 reduce-scatter.6.cloned.1.call-done.refs_1_
  941.8 52.9 %reduce-scatter.8.cloned.1.call-done.refs_2_ = f32[1536,128]{1,0:T(8,128)} async-done(((f32[12288,128]{1,0:T(8,128)}), f32[1536,128]{1,0:T(8,128)}) %reduce-scatter.8.cloned.1.call-update) | async-done | bytes 786448 | tf_op jit(solution)/shard_map/reduce_scatter | solution.py:297
  994.8 5.2 assemble.1
Async XLA Ops:
  7.2 39.0 %all-gather.5.cloned.1.call-start = ((), (), s32[]{:S(2)}) async-start(), calls=%async_computation.3 | async-start | bytes 5308416 | tf_op jit(solution)/shard_map/all_gather | solution.py:293
  9.2 126.1 %all-gather.7.cloned.1.call-start = ((), (), s32[]{:S(2)}) async-start(), calls=%async_computation.4 | async-start | bytes 5308416 | tf_op jit(solution)/shard_map/all_gather | solution.py:293
  46.2 194.6 %all-gather.9.cloned.1.call-start = ((), (), s32[]{:S(2)}) async-start(), calls=%async_computation.5 | async-start | bytes 5308416 | tf_op jit(solution)/shard_map/all_gather | solution.py:293
  134.7 106.1 %all-gather.11.cloned.1.call-start = ((), (), s32[]{:S(2)}) async-start(), calls=%async_computation.6 | async-start | bytes 5308416 | tf_op jit(solution)/shard_map/all_gather | solution.py:293
  135.2 711.0 %reduce-scatter.4.cloned.1.call-start = ((), (), s32[]{:S(2)}) async-start(), calls=%async_computation.7 | async-start | bytes 21233664 | tf_op jit(solution)/shard_map/reduce_scatter | solution.py:297
  663.0 278.8 %reduce-scatter.6.cloned.1.call-start = ((), (), s32[]{:S(2)}) async-start(), calls=%async_computation.8 | async-start | bytes 14155776 | tf_op jit(solution)/shard_map/reduce_scatter | solution.py:297
  846.2 148.6 %reduce-scatter.8.cloned.1.call-start = ((), (), s32[]{:S(2)}) async-start(), calls=%async_computation.9 | async-start | bytes 7077888 | tf_op jit(solution)/shard_map/reduce_scatter | solution.py:297
Sparse Core Ops, SparseCore 0:
  10.4 35.7 all-gather.4
  48.5 32.9 all-gather.6
  134.8 32.9 all-gather.8
  169.4 32.9 all-gather.10
  663.2 117.0 reduce-scatter.3
  846.3 82.4 reduce-scatter.5
  941.9 52.7 reduce-scatter.7

commit v2 on v1

--- a/solution.py
+++ b/solution.py
@@ -85,35 +85,35 @@
     return pieces[0] if len(pieces) == 1 else jnp.concatenate(pieces, 0)
 
 
-def residual_kernel(tile, block, parts, x_ref, h_ref, w_ref, y_ref, total_scr):
+def residual_kernel(tile, block, parts, x_ref, *refs):
+    h_refs = refs[:len(parts)]
+    w_ref, y_ref, total_scr = refs[len(parts):]
     owners = w_ref.shape[0]
-    base = 0
-    for lo, up in parts:
-        hid = owners * (up - lo)
-        for c in range(hid // block):
-            cols = pl.ds(base + c * block, block)
+    fresh = True
+    for h_ref, (lo, up) in zip(h_refs, parts):
+        for c in range(owners * (up - lo) // block):
+            cols = pl.ds(c * block, block)
             active = jnp.concatenate(
                 [gelu_value(h_ref[pl.ds(r * ROW_BLOCK, ROW_BLOCK), cols]) for r in range(tile // ROW_BLOCK)], 0)
             part = dot(active, part_rows(w_ref, lo, up, c * block, block))
-            if base + c == 0:
+            if fresh:
                 total_scr[...] = part
             else:
                 total_scr[...] += part
-        base += hid
+            fresh = False
     y_ref[...] = x_ref[...] + total_scr[...].astype(BF)
 
 
-def residual_of(x, h, w, parts, tile, block):
+def residual_of(x, h_parts, w, parts, tile, block):
     tokens, width = x.shape
-    hid = h.shape[1]
-    return call(
-        functools.partial(residual_kernel, tile, block, parts), "residual", tokens * width * hid,
+    return call(
+        functools.partial(residual_kernel, tile, block, parts), "residual", tokens * width * w.shape[0] * w.shape[1],
         grid=(tokens // tile,),
-        in_specs=[rows_of(width, tile), rows_of(hid, tile), resident(w.shape)],
+        in_specs=[rows_of(width, tile)] + [rows_of(h.shape[1], tile) for h in h_parts] + [resident(w.shape)],
         out_specs=rows_of(width, tile),
         out_shape=jax.ShapeDtypeStruct(x.shape, BF),
         scratch_shapes=[pltpu.VMEM((tile, width), F32)],
-    )(x, h, w)
+    )(x, *h_parts, w)
 
 
 def row_blocks(value):
@@ -233,7 +233,7 @@
     flush(g_in_acc, g_out_acc, grads_out, sems)
 
 
-def bottom_part(x, e, h, w2, part, first, tile, block):
+def bottom_part(x, e, h, w2, part, tile, block):
     tokens, width = x.shape
     owners = w2.shape[0]
     hid = owners * (part[1] - part[0])
@@ -241,30 +241,29 @@
     return call(
         functools.partial(bottom_kernel, tile, block, part), "bottom_part", 3 * tokens * width * hid,
         grid=(tokens // tile,),
-        in_specs=[rows_of(width, tile), rows_of(width, tile), pl.BlockSpec((tile, hid), lambda i: (i, first // hid)), resident(w2.shape)],
+        in_specs=[rows_of(width, tile), rows_of(width, tile), rows_of(hid, tile), resident(w2.shape)],
         out_specs=pl.BlockSpec(memory_space=pl.ANY),
         out_shape=out,
         scratch_shapes=scratch,
     )(x, e, h, w2)
 
 
-def part_columns_kernel(parts, owners, w_ref, out_ref):
+def part_columns_kernel(parts, owners, w_ref, *out_refs):
     own = w_ref.shape[2] // owners
-    base = 0
-    for lo, up in parts:
+    for out_ref, (lo, up) in zip(out_refs, parts):
         for d in range(owners):
-            out_ref[:, pl.ds(base, up - lo)] = w_ref[0, :, pl.ds(d * own + lo, up - lo)]
-            base += up - lo
+            out_ref[:, pl.ds(d * (up - lo), up - lo)] = w_ref[0, :, pl.ds(d * own + lo, up - lo)]
 
 
 def part_columns(w, parts, owners):
     _, rows, hid = w.shape
+    widths = [owners * (up - lo) for lo, up in parts]
     return call(
         functools.partial(part_columns_kernel, parts, owners), "part_columns", rows * hid,
         grid=(1,),
         in_specs=[pl.BlockSpec((1, rows, hid), lambda i: (0, 0, 0))],
-        out_specs=resident((rows, hid)),
-        out_shape=jax.ShapeDtypeStruct((rows, hid), w.dtype),
+        out_specs=[resident((rows, wide)) for wide in widths],
+        out_shape=[jax.ShapeDtypeStruct((rows, wide), w.dtype) for wide in widths],
     )(w)
 
 
@@ -311,19 +310,21 @@
         e2 = cot_loc.reshape(tokens, width)
 
         parts = ((0, own - 128), (own - 128, own))
-        w1 = gather(part_columns(w_in_loc, parts, owners))
-        w1, first_out = lax.optimization_barrier((w1, w_out_loc[0]))
-        w2 = gather(first_out)
-        h0 = hidden_of(x0, w1, 1024)
-        later_in, later_out, h0 = lax.optimization_barrier((w_in_loc[1], w_out_loc[1], h0))
+        w1_large, w1_small = part_columns(w_in_loc, parts, owners)
+        w1_small, w1_large = lax.optimization_barrier((gather(w1_small), w1_large))
+        w1_large = gather(w1_large)
+        h_small = hidden_of(x0, w1_small, 2048)
+        w1_large, first_out, h_small = lax.optimization_barrier((w1_large, w_out_loc[0], h_small))
+        w2 = gather(first_out).reshape(owners, own, width)
+        h_large = hidden_of(x0, w1_large, 1024)
+        later_in, later_out, h_large = lax.optimization_barrier((w_in_loc[1], w_out_loc[1], h_large))
         w1_top, w2_top = gather(later_in), gather(later_out)
-        w2 = w2.reshape(owners, own, width)
-        x1 = residual_of(x0, h0, w2, parts, 512, 1024)
-        e1, top = top_layer(x1, e2, w1_top, w2_top, owners, 512, 1024)
+        x1 = residual_of(x0, (h_large, h_small), w2, parts, 512, 1024)
+        e1, top = top_layer(x1, e2, w1_top, w2_top, owners, 512, 1536)
         top = scatter_sum(top)
-        large = scatter_sum(bottom_part(x0, e1, h0, w2, parts[0], 0, 1024, 512))
+        large = scatter_sum(bottom_part(x0, e1, h_large, w2, parts[0], 1024, 512))
         e1, top = lax.optimization_barrier((e1, top))
-        small = scatter_sum(bottom_part(x0, e1, h0, w2, parts[1], hid - owners * 128, 1024, 256))
+        small = scatter_sum(bottom_part(x0, e1, h_small, w2, parts[1], 1024, 256))
         places = ((1, 0, own), (0, *parts[0]), (0, *parts[1]))
         return assemble(places, (top, large, small), rows, hid, own, width)
 

time: 1010 us -> 1010 us (level)
  waiting for transfers between devices: 88.2 us -> 77.4 us
    all_gather x4 -> x5, waiting for transfers between devices: 34.6 us -> 23.8 us  [gather(): return lax.all_gather(rows, GROUP_AXIS, axis=0, tiled=True)]
    pallas_call x1 -> x2, Pallas kernels: 86.5 us -> 91.2 us  [hidden_of(): call(hidden_kernel, 'hidden', tokens * width * hid, grid=(tokens // tile,...]
  transfers between devices with their start and end apart: 7 -> 8, of which waited for: 2 -> 2; matrix products, arithmetic and copies ran while one was open for 0% -> 0% of each run, Pallas kernels for 47% -> 48%
where the time goes in v2:
time: 1010 us; the launch traced here: 1000 us
  Pallas kernels  903 us (89%)
  waiting for transfers between devices  77.4 us (8%)
  between operations  14.6 us (1%)
    pallas_call x1, Pallas kernels, top_layer(): call(functools.partial(top_kernel, tile, block), 'top_layer', 5 * tokens...  421 us
    pallas_call x2, Pallas kernels, bottom_part(): call(functools.partial(bottom_kernel, tile, block, part), 'bottom_part',...  278 us
    pallas_call x1, Pallas kernels, residual_of(): call(functools.partial(residual_kernel, tile, block, parts), 'residual',...  106 us
    pallas_call x2, Pallas kernels, hidden_of(): call(hidden_kernel, 'hidden', tokens * width * hid, grid=(tokens // tile,...  91.2 us
    reduce_scatter x3, waiting for transfers between devices, scatter_sum(): lax.psum_scatter(grads.reshape(-1, grads.shape[-1]), GROUP_AXIS, scatter_...  52.9 us
    all_gather x5, waiting for transfers between devices, gather(): return lax.all_gather(rows, GROUP_AXIS, axis=0, tiled=True)  23.8 us
  transfers between devices with their start and end apart: 8, of which 2 were waited for; matrix products, arithmetic and copies ran while one was open for 0% of the time, Pallas kernels for 48%

profile of v2, /device:TPU:0, one launch (start us, length us, event | category | flops | bytes accessed | tf_op | source)
XLA Modules:
  0.0 999.6 jit_solution(18328803478820313202)
XLA Ops:
  7.2 0.0 all-gather.6.cloned.1.call-start
  7.2 1.9 part_columns.1
  9.1 0.0 all-gather.6.cloned.1.call-update
  9.2 0.0 all-gather.8.cloned.1.call-start
  9.2 23.8 %all-gather.6.cloned.1.call-done.w_ref = bf16[768,1024]{1,0:T(8,128)(2,1)} async-done(((bf16[96,1024]{1,0:T(8,128)(2,1)}), bf16[768,1024]{1,0:T(8,128)(2,1)}) %all-gather.6.cloned.1.call-update) | async-done | bytes 1572880 | tf_op jit(solution)/shard_map/all_gather | solution.py:292
  33.0 0.0 all-gather.8.cloned.1.call-update
  33.0 0.0 all-gather.10.cloned.1.call-start
  33.0 2.3 slice_bitcast_fusion
  35.4 31.9 %hidden.2.refs_1_.h_ref = bf16[16384,1024]{1,0:T(8,128)(2,1)} custom-call(bf16[16384,768]{1,0:T(8,128)(2,1)} %bitcast.16, bf16[768,1024]{1,0:T(8,128)(2,1)} %all-gather.6.cloned.1.call-done.w_ref), custom_call_target="tpu_custom_call" | custom-call | flops 25769803776 | bytes 1048576 | tf_op jit(solution)/shard_map/hidden/pallas_call | solution.py:68
  67.3 0.0 all-gather.8.cloned.1.call-done.w_ref
  67.3 0.0 all-gather.10.cloned.1.call-update
  67.3 0.0 all-gather.12.cloned.1.call-start
  67.4 1.9 slice_bitcast_fusion.2
  69.3 59.3 %hidden.3.refs_0_.h_ref = bf16[16384,2048]{1,0:T(8,128)(2,1)} custom-call(bf16[16384,768]{1,0:T(8,128)(2,1)} %bitcast.17, bf16[768,2048]{1,0:T(8,128)(2,1)} %all-gather.8.cloned.1.call-done.w_ref), custom_call_target="tpu_custom_call" | custom-call | flops 51539607552 | bytes 1048576 | tf_op jit(solution)/shard_map/hidden/pallas_call | solution.py:68
  128.6 0.0 all-gather.12.cloned.1.call-update
  128.6 0.0 all-gather.14.cloned.1.call-start
  128.7 0.5 all-gather.14.cloned.1.call-update
  129.2 0.0 reduce-scatter.4.cloned.1.call-start
  129.3 0.0 all-gather.10.cloned.1.call-done
  129.3 106.0 %residual.1.x_ref = bf16[16384,768]{1,0:T(8,128)(2,1)} custom-call(bf16[16384,768]{1,0:T(8,128)(2,1)} %bitcast.18, bf16[16384,2048]{1,0:T(8,128)(2,1)} %hidden.3.refs_0_.h_ref, bf16[16384,1024]{1,0:T(8,128)(2,1)} %hidden.2.refs_1_.h_ref, bf16[8,384,768]{2,1,0:T(8,128)(2,1)} %bitcast.21), custom_call_target="tpu_custom_call" | custom-call | flops 77309411328 | bytes 1048576 | tf_op jit(solution)/shard_map/residual/pallas_call | solution.py:109
  235.3 0.0 all-gather.12.cloned.1.call-done.w1_ref
  235.3 0.0 all-gather.14.cloned.1.call-done.w2_ref
  235.3 420.5 %top_layer.1 = (bf16[16384,768]{1,0:T(8,128)(2,1)}, f32[8,2,768,384]{3,2,1,0:T(8,128)}) custom-call(bf16[16384,768]{1,0:T(8,128)(2,1)} %residual.1.x_ref, bf16[16384,768]{1,0:T(8,128)(2,1)} %bitcast.15, bf16[768,3072]{1,0:T(8,128)(2,1)} %all-gather.12.cloned.1.call-done.w1_ref, ...), custom_call_target="tpu_custom_call", output_to_operand_aliasing={{0}: (0, {})} | custom-call | flops 386547056640 | bytes 1048576 | tf_op jit(solution)/shard_map/top_layer/pallas_call | solution.py:207
  655.8 0.0 reduce-scatter.4.cloned.1.call-update
  655.8 0.0 reduce-scatter.6.cloned.1.call-start
  655.9 182.6 %bottom_part.2 = f32[8,2,768,256]{3,2,1,0:T(8,128)} custom-call(bf16[16384,768]{1,0:T(8,128)(2,1)} %bitcast.19, bf16[16384,768]{1,0:T(8,128)(2,1)} %get-tuple-element.29.e_ref, bf16[16384,2048]{1,0:T(8,128)(2,1)} %hidden.3.refs_0_.h_ref, bf16[8,384,768]{2,1,0:T(8,128)(2,1)} %bitcast.22), custom_call_target="tpu_custom_call" | custom-call | flops 154618822656 | bytes 1048576 | tf_op jit(solution)/shard_map/bottom_part/pallas_call | solution.py:241
  838.5 0.0 reduce-scatter.6.cloned.1.call-update
  838.5 0.0 reduce-scatter.8.cloned.1.call-start
  838.6 0.0 reduce-scatter.4.cloned.1.call-done.refs_0_
  838.6 95.5 %bottom_part.3 = f32[8,2,768,128]{3,2,1,0:T(8,128)} custom-call(bf16[16384,768]{1,0:T(8,128)(2,1)} %bitcast.20, bf16[16384,768]{1,0:T(8,128)(2,1)} %get-tuple-element.29.e_ref, bf16[16384,1024]{1,0:T(8,128)(2,1)} %hidden.2.refs_1_.h_ref, bf16[8,384,768]{2,1,0:T(8,128)(2,1)} %bitcast.23), custom_call_target="tpu_custom_call" | custom-call | flops 77309411328 | bytes 1048576 | tf_op jit(solution)/shard_map/bottom_part/pallas_call | solution.py:241
  934.1 0.0 reduce-scatter.8.cloned.1.call-update
  934.2 0.0 reduce-scatter.6.cloned.1.call-done.refs_1_
  934.2 52.9 %reduce-scatter.8.cloned.1.call-done.refs_2_ = f32[1536,128]{1,0:T(8,128)} async-done(((f32[12288,128]{1,0:T(8,128)}), f32[1536,128]{1,0:T(8,128)}) %reduce-scatter.8.cloned.1.call-update) | async-done | bytes 786448 | tf_op jit(solution)/shard_map/reduce_scatter | solution.py:296
  987.1 5.2 assemble.1
Async XLA Ops:
  7.2 25.8 %all-gather.6.cloned.1.call-start = ((), (), s32[]{:S(2)}) async-start(), calls=%async_computation.3 | async-start | bytes 1769472 | tf_op jit(solution)/shard_map/all_gather | solution.py:292
  9.2 58.2 %all-gather.8.cloned.1.call-start = ((), (), s32[]{:S(2)}) async-start(), calls=%async_computation.4 | async-start | bytes 3538944 | tf_op jit(solution)/shard_map/all_gather | solution.py:292
  33.0 96.3 %all-gather.10.cloned.1.call-start = ((), (), s32[]{:S(2)}) async-start(), calls=%async_computation.5 | async-start | bytes 5308416 | tf_op jit(solution)/shard_map/all_gather | solution.py:292
  67.3 167.9 %all-gather.12.cloned.1.call-start = ((), (), s32[]{:S(2)}) async-start(), calls=%async_computation.6 | async-start | bytes 5308416 | tf_op jit(solution)/shard_map/all_gather | solution.py:292
  128.6 106.7 %all-gather.14.cloned.1.call-start = ((), (), s32[]{:S(2)}) async-start(), calls=%async_computation.7 | async-start | bytes 5308416 | tf_op jit(solution)/shard_map/all_gather | solution.py:292
  129.2 709.4 %reduce-scatter.4.cloned.1.call-start = ((), (), s32[]{:S(2)}) async-start(), calls=%async_computation.8 | async-start | bytes 21233664 | tf_op jit(solution)/shard_map/reduce_scatter | solution.py:296
  655.8 278.4 %reduce-scatter.6.cloned.1.call-start = ((), (), s32[]{:S(2)}) async-start(), calls=%async_computation.9 | async-start | bytes 14155776 | tf_op jit(solution)/shard_map/reduce_scatter | solution.py:296
  838.5 148.6 %reduce-scatter.8.cloned.1.call-start = ((), (), s32[]{:S(2)}) async-start(), calls=%async_computation.10 | async-start | bytes 7077888 | tf_op jit(solution)/shard_map/reduce_scatter | solution.py:296
Sparse Core Ops, SparseCore 0:
  10.4 22.5 all-gather.5
  34.8 26.3 all-gather.7
  67.5 32.9 all-gather.9
  128.7 32.9 all-gather.11
  163.9 32.9 all-gather.13
  655.9 117.0 reduce-scatter.3
  838.6 82.4 reduce-scatter.5
  934.3 52.7 reduce-scatter.7
